TPU v7x, 32 devices: a whole 2x2x4 slice. The times are simulated.
32 devices in a mesh: tile: 8 (over z, y), mem: 4 (over x, core).
Axes of the slice: x: 2, y: 2, z: 4, core: 2. Of those that a mesh axis runs over, the one named last changes fastest.
Arguments:
- background: bfloat16 [112, 80, 512], P('tile', 'mem'), may hold values from -6 to 6
- obs_ens: bfloat16 [112, 80, 128], P('tile', 'mem'), may hold values from -6 to 6
- innovation: float32 [112, 128], P('tile'), may hold values from -6 to 6
- precision: float32 [112, 128], P('tile'), may hold values from 0.1 to 2
- loc_weight: float32 [112, 7], P('tile'), may hold values from 0.1 to 1
- old_split: int32 [9], replicated, may hold values from 0 to 64, as said below
- new_split: int32 [9], replicated, may hold values from 0 to 64, as said below
- obs_count: int32 [112], P('tile'), may hold values from 32 to 128
- halo_tiles: int32 [8, 12], replicated, may hold values from 0 to 63, as said below
- region_list: int32 [112, 7], P('tile'), may hold values from 0 to 25, as said below
Outputs:
- analysis: bfloat16 [112, 80, 512], P('tile', 'mem')
Inputs may be any that keep to these rules, and one draw needn't show every extreme that they name: old_split[0] = 0 and old_split[8] = 64; each device holds between 2 and 14 old tiles, exactly 14 on some device. new_split[0] = 0 and new_split[8] = 64; each device holds between 6 and 10 new tiles; every new_split[d] differs from old_split[d] by at most 2, by exactly 2 for some d. `halo_tiles`: row d is 3 groups of 4 entries; a group holds distinct tiles in rising order that one device p other than d holds under new_split, with p within 3 of d, and the 3 devices of a row are distinct. `region_list`: for a slot of device d, an entry r < 14 names d's slot r, which is live; an entry r >= 14 names the tile halo_tiles[d, r - 14].
All inputs are finite; a program needn't handle non-finite values.
Results may differ from a plain program's by a relative error of at most 0.0057.
Values may be sent and summed in bfloat16 or wider, within the bound.
A program may use at most 64 MiB of HBM per device.

v0:
```python
import functools
import math

import jax
import jax.numpy as jnp
from jax import lax
from jax.experimental import pallas as pl
from jax.experimental.pallas import tpu as pltpu
from jax.sharding import PartitionSpec as P

TILE_MEAN = 8
MOVE = 2
REACH = 3
HPEER = 3
HCAP = 4
NS_ITERS = 6
LIVE_MAX = TILE_MEAN + MOVE
INFLATION = 1.1
PAD = 24
MESH = pl.DeviceIdType.MESH
F32 = jnp.float32
BF16 = jnp.bfloat16
OFFSETS = tuple(range(-REACH, 0)) + tuple(range(1, REACH + 1))


def dot(a, b):
    return jnp.dot(a, b, preferred_element_type=F32)


def cut(a):
    high = a.astype(BF16)
    return high, (a - high.astype(F32)).astype(BF16)


def dot3(a, b):
    ah, al = a
    bh, bl = b
    return dot(ah, bh) + (dot(ah, bl) + dot(al, bh))


def kernel(
    devices,
    ranks,
    old_ref,
    new_ref,
    count_ref,
    halo_ref,
    region_ref,
    weight_ref,
    back_ref,
    obs_ref,
    innov_ref,
    prec_ref,
    out_ref,
    mine,
    back_t,
    table,
    stage,
    arrived,
    mig_out,
    mig_in,
    states,
    gram_s,
    y_s,
    z_s,
    t_out,
    t_in,
    halo_send,
    halo_recv,
    mig_send,
    mig_recv,
    own_send,
    own_recv,
    far_send,
    far_recv,
    state_send,
    state_recv,
    t_send,
    t_recv,
):
    members, capacity, width = back_ref.shape
    obs_slots = obs_ref.shape[2]
    ensemble = members * ranks
    full = PAD * ranks
    halo_count = HPEER * HCAP
    per_rank = -(-LIVE_MAX // ranks)
    me = lax.axis_index("tile")
    rank = lax.axis_index("mem")
    peers = [lax.rem(rank + j, ranks) for j in range(1, ranks)]

    barrier = pltpu.get_barrier_semaphore()
    for offset in OFFSETS:
        target = me + offset

        @pl.when((target >= 0) & (target < devices))
        def _():
            pl.semaphore_signal(barrier, inc=1, device_id=(target, rank), device_id_type=MESH)

    for peer in peers:
        pl.semaphore_signal(barrier, inc=1, device_id=(me, peer), device_id_type=MESH)

    old_start, old_end = old_ref[me], old_ref[me + 1]
    new_start, new_end = new_ref[me], new_ref[me + 1]
    row_id = lax.broadcasted_iota(jnp.int32, (PAD, obs_slots), 0)
    lane_id = lax.broadcasted_iota(jnp.int32, (1, obs_slots), 1)

    obs_all = obs_ref[...].astype(F32)
    for s in range(LIVE_MAX):
        live = (lane_id < count_ref[s]).astype(F32)
        root = jnp.sqrt(prec_ref[s : s + 1, :] * live)
        pulled = root * innov_ref[s : s + 1, :]
        rows = obs_all[:, s, :] * root
        fill = jnp.zeros((PAD - members, obs_slots), F32)
        block = jnp.concatenate([rows, fill], axis=0)
        block = jnp.where(row_id == members, pulled, block).astype(BF16)
        mine[s] = block
        table[s, rank] = block

    for k, offset in enumerate(OFFSETS):
        reader = jnp.clip(me + offset, 0, devices - 1)
        for c in range(HCAP):
            index = jnp.int32(0)
            for g in range(HPEER):
                first = halo_ref[reader, g * HCAP]
                here = (first >= new_start) & (first < new_end)
                index += jnp.where(here, halo_ref[reader, g * HCAP + c] - new_start, 0)
            index = jnp.clip(index, 0, LIVE_MAX - 1)
            stage[k, c] = mine[index]

    for s in range(LIVE_MAX):
        states[s, rank] = jnp.zeros((PAD, width), BF16)

    signals = ranks - 1
    for offset in OFFSETS:
        inside = (me + offset >= 0) & (me + offset < devices)
        signals += jnp.where(inside, 1, 0)
    pl.semaphore_wait(barrier, signals)

    def remote(src, dst, send, recv, target):
        return pltpu.make_async_remote_copy(
            src_ref=src,
            dst_ref=dst,
            send_sem=send,
            recv_sem=recv,
            device_id=target,
            device_id_type=MESH,
        )

    halo_copies = []
    for k, offset in enumerate(OFFSETS):
        target = me + offset
        back_slot = len(OFFSETS) - 1 - k
        copy = remote(
            stage.at[k], arrived.at[back_slot], halo_send.at[k], halo_recv.at[back_slot],
            (target, rank),
        )
        source = me + OFFSETS[back_slot]
        halo_copies.append(copy)

        @pl.when((target >= 0) & (target < devices))
        def _(copy=copy):
            copy.start()

    own_rows = pl.ds(0, LIVE_MAX)
    far_rows = pl.ds(LIVE_MAX, halo_count)
    pair = rank + 1 - 2 * lax.rem(rank, 2)
    half_ranks = ranks // 2

    def gather(piece, send, recv):
        here = piece(rank)
        direct = [remote(here, here, send.at[0], recv.at[0], (me, pair))]
        passed = []
        for j in range(1, half_ranks):
            ahead = lax.rem(rank + 2 * j, ranks)
            behind = piece(lax.rem(rank + ranks - 2 * j, ranks))
            direct.append(remote(here, here, send.at[j], recv.at[j], (me, ahead)))
            k = half_ranks + j - 1
            passed.append(remote(behind, behind, send.at[k], recv.at[k], (me, pair)))
        return direct, passed

    def start(copies):
        for copy in copies:
            copy.start()

    def arrive(copies):
        for copy in copies:
            copy.wait_recv()

    own_copies, own_passed = gather(lambda r: table.at[own_rows, r], own_send, own_recv)
    far_copies, far_passed = gather(lambda r: table.at[far_rows, r], far_send, far_recv)
    state_copies, state_passed = gather(lambda r: states.at[:, r], state_send, state_recv)
    start(own_copies[::-1])

    back_all = back_ref[...].astype(F32)
    for s in range(capacity):
        back_t[s] = back_all[:, s, :].astype(BF16)
    old_count = old_end - old_start
    for c in range(MOVE):
        mig_out[0, c] = back_t[jnp.clip(c, 0, capacity - 1)]
        mig_out[1, c] = back_t[jnp.clip(old_count - MOVE + c, 0, capacity - 1)]
    mig_copies = []
    for side, offset in ((0, -1), (1, 1)):
        target = me + offset
        copy = remote(
            mig_out.at[side], mig_in.at[1 - side], mig_send.at[side], mig_recv.at[1 - side],
            (target, rank),
        )
        mig_copies.append(copy)

        @pl.when((target >= 0) & (target < devices))
        def _(copy=copy):
            copy.start()

    for k, offset in enumerate(OFFSETS):
        back_slot = len(OFFSETS) - 1 - k
        source = me + OFFSETS[back_slot]

        @pl.when((source >= 0) & (source < devices))
        def _(copy=halo_copies[k]):
            copy.wait_recv()

    for g in range(HPEER):
        first = halo_ref[me, g * HCAP]
        owner = jnp.int32(0)
        for k, offset in enumerate(OFFSETS):
            source = jnp.clip(me + offset, 0, devices - 1)
            held = (first >= new_ref[source]) & (first < new_ref[source + 1])
            inside = (me + offset >= 0) & (me + offset < devices)
            owner = jnp.where(held & inside, k, owner)
        for c in range(HCAP):
            table[LIVE_MAX + g * HCAP + c, rank] = arrived[owner, c]
    start(far_copies[::-1])

    for side, offset in ((0, -1), (1, 1)):
        source = me - offset

        @pl.when((source >= 0) & (source < devices))
        def _(copy=mig_copies[side]):
            copy.wait_recv()

    for s in range(LIVE_MAX):
        position = new_start + s
        left = mig_in[0, jnp.clip(position - old_start + MOVE, 0, MOVE - 1)]
        own = back_t[jnp.clip(position - old_start, 0, capacity - 1)]
        right = mig_in[1, jnp.clip(position - old_end, 0, MOVE - 1)]
        row = jnp.where(position < old_start, left, jnp.where(position < old_end, own, right))
        states[s, rank, :members] = row
    start(state_copies[::-1])

    arrive(own_copies[1:])
    start(own_passed)
    arrive(far_copies[1:])
    start(far_passed)
    arrive(own_copies[:1] + own_passed + far_copies[:1] + far_passed)

    grid_row = lax.broadcasted_iota(jnp.int32, (full, full), 0)
    grid_col = lax.broadcasted_iota(jnp.int32, (full, full), 1)
    live_row = lax.rem(grid_row, PAD) < members
    live_col = lax.rem(grid_col, PAD) < members
    unit = (grid_row == grid_col).astype(F32)
    live_unit = jnp.where(live_row, unit, 0.0)
    line = lax.broadcasted_iota(jnp.int32, (1, full), 1)
    live_line = lax.rem(line, PAD) < members
    shift = (ensemble - 1) / INFLATION
    entries = region_ref.shape[0] + 1

    norms, pulls = [], []
    for b in range(per_rank):
        slot = jnp.minimum(rank + b * ranks, LIVE_MAX - 1)
        gram = jnp.zeros((full, full), F32)
        for e in range(entries):
            if e == 0:
                index = slot
            else:
                named = region_ref[e - 1, slot]
                index = jnp.where(named < capacity, named, named - capacity + LIVE_MAX)
            index = jnp.clip(index, 0, LIVE_MAX + halo_count - 1)
            block = table[index].reshape(full, obs_slots)
            product = lax.dot_general(
                block, block, (((1,), (1,)), ((), ())), preferred_element_type=F32
            )
            gram += product if e == 0 else weight_ref[e - 1, slot] * product
        pulls.append(jnp.where(live_line, gram[members : members + 1, :], 0.0))
        system = jnp.where(live_row & live_col, gram, 0.0) + shift * live_unit
        total = jnp.sum(jnp.sum(system * system, axis=1, keepdims=True), axis=0, keepdims=True)
        norm = jnp.sqrt(total)
        norms.append(norm)
        y = system / norm
        middle = 1.5 * unit - 0.5 * y
        y_s[b] = dot3(cut(y), cut(middle))
        z_s[b] = middle

    def step(_, carry):
        middles = []
        for b in range(per_rank):
            middles.append(cut(1.5 * unit - 0.5 * dot3(cut(z_s[b]), cut(y_s[b]))))
        for b in range(per_rank):
            y_s[b] = dot3(cut(y_s[b]), middles[b])
            z_s[b] = dot3(middles[b], cut(z_s[b]))
        return carry

    lax.fori_loop(0, NS_ITERS - 2, step, 0)
    for b in range(per_rank):
        z = cut(z_s[b])
        middle = cut(1.5 * unit - 0.5 * dot3(z, cut(y_s[b])))
        inverse = dot3(middle, z)
        parts = cut(inverse)
        pull = jnp.broadcast_to(pulls[b], (8, full))
        half = dot3(cut(pull), parts)
        shift_row = dot3(cut(half), parts)[:1] / norms[b]
        spread = math.sqrt(ensemble - 1) * lax.rsqrt(norms[b])
        transposed = spread * inverse + jnp.where(live_line, shift_row, 0.0)
        t_out[b] = transposed.astype(BF16).reshape(ranks, PAD, full)

    t_copies = []
    for j, peer in enumerate(peers):
        copy = remote(
            t_out.at[:, peer], t_in.at[rank], t_send.at[j], t_recv.at[j], (me, peer)
        )
        t_copies.append(copy)
        copy.start()
    t_in[rank] = t_out[:, rank]

    arrive(state_copies[1:])
    start(state_passed)
    arrive(t_copies + state_copies[:1] + state_passed)

    piece_row = lax.broadcasted_iota(jnp.int32, (PAD, full), 0)
    for s in range(LIVE_MAX):
        weights = t_in[s % ranks, s // ranks]
        weights = jnp.where(piece_row == members, jnp.ones_like(weights), weights)
        keep = 1.0 - jnp.sum(weights.astype(F32), axis=1, keepdims=True)
        blended = dot(weights, states[s].reshape(full, width))
        mean = blended[members : members + 1, :] / ensemble
        value = (blended + keep * mean)[:members]
        is_live = new_start + s < new_end
        out_ref[s] = jnp.where(is_live, value, 0.0).astype(BF16)
    for s in range(LIVE_MAX, capacity):
        out_ref[s] = jnp.zeros((members, width), BF16)

    for k, offset in enumerate(OFFSETS):
        target = me + offset

        @pl.when((target >= 0) & (target < devices))
        def _(copy=halo_copies[k]):
            copy.wait_send()

    for side, offset in ((0, -1), (1, 1)):
        target = me + offset

        @pl.when((target >= 0) & (target < devices))
        def _(copy=mig_copies[side]):
            copy.wait_send()

    gathers = own_copies + own_passed + far_copies + far_passed + state_copies + state_passed
    for copy in gathers + t_copies:
        copy.wait_send()


def shards(devices, ranks, background, obs_ens, innovation, precision, loc_weight, old_split,
           new_split, obs_count, halo_tiles, region_list):
    capacity, members, width = background.shape
    obs_slots = obs_ens.shape[2]
    full = PAD * ranks
    halo_count = HPEER * HCAP
    per_rank = -(-LIVE_MAX // ranks)
    smem = pl.BlockSpec(memory_space=pltpu.SMEM)
    vmem = pl.BlockSpec(memory_space=pltpu.VMEM)
    count = len(OFFSETS)
    dma = pltpu.SemaphoreType.DMA
    return pl.pallas_call(
        functools.partial(kernel, devices, ranks),
        out_shape=jax.ShapeDtypeStruct((capacity, members, width), BF16),
        in_specs=[smem] * 6 + [vmem] * 4,
        out_specs=vmem,
        scratch_shapes=[
            pltpu.VMEM((LIVE_MAX, PAD, obs_slots), BF16),
            pltpu.VMEM((capacity, members, width), BF16),
            pltpu.VMEM((LIVE_MAX + halo_count, ranks, PAD, obs_slots), BF16),
            pltpu.VMEM((count, HCAP, PAD, obs_slots), BF16),
            pltpu.VMEM((count, HCAP, PAD, obs_slots), BF16),
            pltpu.VMEM((2, MOVE, members, width), BF16),
            pltpu.VMEM((2, MOVE, members, width), BF16),
            pltpu.VMEM((LIVE_MAX, ranks, PAD, width), BF16),
            pltpu.VMEM((per_rank, full, full), F32),
            pltpu.VMEM((per_rank, full, full), F32),
            pltpu.VMEM((per_rank, full, full), F32),
            pltpu.VMEM((per_rank, ranks, PAD, full), BF16),
            pltpu.VMEM((ranks, per_rank, PAD, full), BF16),
            dma((count,)),
            dma((count,)),
            dma((2,)),
            dma((2,)),
            dma((ranks - 1,)),
            dma((ranks - 1,)),
            dma((ranks - 1,)),
            dma((ranks - 1,)),
            dma((ranks - 1,)),
            dma((ranks - 1,)),
            dma((ranks - 1,)),
            dma((ranks - 1,)),
        ],
        compiler_params=pltpu.CompilerParams(collective_id=0, has_side_effects=True),
        cost_estimate=pl.CostEstimate(flops=10**8, bytes_accessed=10**7, transcendentals=0),
    )(old_split, new_split, obs_count, halo_tiles, region_list.T, loc_weight.T,
      jnp.swapaxes(background, 0, 1), jnp.swapaxes(obs_ens, 0, 1), innovation, precision)


def solution(mesh):
    in_specs = (
        P("tile", "mem", None),
        P("tile", "mem", None),
        P("tile", None),
        P("tile", None),
        P("tile", None),
        P(),
        P(),
        P("tile"),
        P(),
        P("tile", None),
    )
    out_specs = P("tile", "mem", None)
    body = functools.partial(shards, mesh.shape["tile"], mesh.shape["mem"])
    return jax.shard_map(body, mesh=mesh, in_specs=in_specs, out_specs=out_specs, check_vma=False)
```

profile of v0, /device:TPU:0, one launch (start us, length us, event | category | flops | bytes accessed | tf_op | source)
XLA Modules:
  0.0 24.4 jit_solution(4880616280085637036)
XLA Ops:
  0.0 22.6 %shard_map.100 = bf16[14,20,512]{2,1,0:T(8,128)(2,1)} custom-call(s32[9]{0:T(128)} %old_ref.1, s32[9]{0:T(128)} %new_ref.1, s32[14]{0:T(128)} %count_ref.1, s32[8,12]{1,0:T(8,128)} %halo_ref.1, s32[7,14]{1,0:T(8,128)} %bitcast.6, f32[7,14]{1,0:T(8,128)} %bitcast.7, bf16[20,14,512]{2,1,0:T(8,128)(2,1)} %bitcast.4, bf16[20,14,128]{2,1,0:T(8,128)(2,1)} %bitcast.5, ...), custom_call_target="tpu_custom_call" | custom-call | flops 100000000 | bytes 10000000 | tf_op jit(solution)/shard_map/pallas_call | solution.py:371
  22.6 1.8 %copy.11 = bf16[14,20,512]{2,0,1:T(8,128)(2,1)} copy(bf16[14,20,512]{2,1,0:T(8,128)(2,1)} %shard_map.100) | data formatting | bytes 573440 | tf_op jit(solution)/shard_map/pallas_call | solution.py:371
where the time goes:
time: 24.6 us; the launch traced here: 24.4 us
  Pallas kernels  22.6 us (92%)
  local copies, waits for them, and re-layouts  1.79 us (7%)
    pallas_call x1, Pallas kernels, shards(): pl.pallas_call(functools.partial(kernel, devices, ranks), out_shape=jax.S...  22.6 us
    pallas_call x1, local copies, waits for them, and re-layouts, shards(): pl.pallas_call(functools.partial(kernel, devices, ranks), out_shape=jax.S...  1.79 us

commit v1 on v0

v1 whole, which is shorter than its diff:
```python
import functools
import math

import jax
import jax.numpy as jnp
from jax import lax
from jax.experimental import pallas as pl
from jax.experimental.pallas import tpu as pltpu
from jax.sharding import PartitionSpec as P

TILE_MEAN = 8
CORES = 2
MOVE = 2
REACH = 3
HPEER = 3
HCAP = 4
NS_ITERS = 6
LIVE_MAX = TILE_MEAN + MOVE
INFLATION = 1.1
PAD = 24
MESH = pl.DeviceIdType.MESH
F32 = jnp.float32
BF16 = jnp.bfloat16
LANES = 128
OFFSETS = tuple(range(-REACH, 0)) + tuple(range(1, REACH + 1))


def dot(a, b):
    return jnp.dot(a, b, preferred_element_type=F32)


def cut(a):
    high = a.astype(BF16)
    return high, (a - high.astype(F32)).astype(BF16)


def kernel(
    devices,
    ranks,
    old_hbm,
    new_hbm,
    count_hbm,
    halo_hbm,
    region_hbm,
    weight_hbm,
    back_hbm,
    obs_hbm,
    innov_hbm,
    prec_hbm,
    out_ref,
    old_ref,
    new_ref,
    count_ref,
    halo_ref,
    region_ref,
    weight_ref,
    back_ref,
    obs_ref,
    innov_ref,
    prec_ref,
    mine,
    back_t,
    table,
    stage,
    arrived,
    mig_out,
    mig_in,
    states,
    gram_s,
    yz_s,
    t_full,
    t_all,
    load_sem,
    halo_send,
    halo_recv,
    mig_send,
    mig_recv,
    own_send,
    own_recv,
    far_send,
    far_recv,
    early_send,
    early_recv,
    state_send,
    state_recv,
    t_send,
    t_recv,
):
    members, capacity, width = back_ref.shape
    obs_slots = obs_ref.shape[2]
    ensemble = members * ranks
    full = PAD * ranks
    halo_count = HPEER * HCAP
    per_core = -(-LIVE_MAX // CORES)
    me = lax.axis_index("tile")
    rank = lax.axis_index("mem")
    core = lax.rem(rank, CORES)
    chip = rank // CORES
    pair = rank + 1 - 2 * core
    half_ranks = ranks // CORES
    peers = [lax.rem(rank + j, ranks) for j in range(1, ranks)]

    barrier = pltpu.get_barrier_semaphore()
    for offset in OFFSETS:
        target = me + offset

        @pl.when((target >= 0) & (target < devices))
        def _():
            pl.semaphore_signal(barrier, inc=1, device_id=(target, rank), device_id_type=MESH)

    for peer in peers:
        pl.semaphore_signal(barrier, inc=1, device_id=(me, peer), device_id_type=MESH)

    loads = {}
    for k, (name, src, dst) in enumerate((
        ("count", count_hbm, count_ref),
        ("obs", obs_hbm, obs_ref),
        ("prec", prec_hbm, prec_ref),
        ("innov", innov_hbm, innov_ref),
        ("new", new_hbm, new_ref),
        ("halo", halo_hbm, halo_ref),
        ("back", back_hbm, back_ref),
        ("old", old_hbm, old_ref),
        ("region", region_hbm, region_ref),
        ("weight", weight_hbm, weight_ref),
    )):
        loads[name] = pltpu.make_async_copy(src, dst, load_sem.at[k])
        loads[name].start()

    row_id = lax.broadcasted_iota(jnp.int32, (PAD, obs_slots), 0)
    lane_id = lax.broadcasted_iota(jnp.int32, (1, obs_slots), 1)

    for s in range(LIVE_MAX):
        states[s, rank] = jnp.zeros((PAD, width), BF16)
    for b in range(per_core):
        yz_s[b, 2 * full :] = jnp.zeros((LANES - full, 2 * LANES), BF16)

    for name in ("count", "obs", "prec", "innov"):
        loads[name].wait()
    obs_all = obs_ref[...].astype(F32)
    for s in range(LIVE_MAX):
        live = (lane_id < count_ref[s]).astype(F32)
        root = jnp.sqrt(prec_ref[s : s + 1, :] * live)
        pulled = root * innov_ref[s : s + 1, :]
        rows = obs_all[:, s, :] * root
        fill = jnp.zeros((PAD - members, obs_slots), F32)
        block = jnp.concatenate([rows, fill], axis=0)
        block = jnp.where(row_id == members, pulled, block).astype(BF16)
        mine[s] = block
        table[s, rank] = block

    loads["new"].wait()
    loads["halo"].wait()
    new_start, new_end = new_ref[me], new_ref[me + 1]
    for k, offset in enumerate(OFFSETS):
        reader = jnp.clip(me + offset, 0, devices - 1)
        for c in range(HCAP):
            index = jnp.int32(0)
            for g in range(HPEER):
                first = halo_ref[reader, g * HCAP]
                here = (first >= new_start) & (first < new_end)
                index += jnp.where(here, halo_ref[reader, g * HCAP + c] - new_start, 0)
            index = jnp.clip(index, 0, LIVE_MAX - 1)
            stage[k, c] = mine[index]

    signals = ranks - 1
    for offset in OFFSETS:
        inside = (me + offset >= 0) & (me + offset < devices)
        signals += jnp.where(inside, 1, 0)
    pl.semaphore_wait(barrier, signals)

    def remote(src, dst, send, recv, target):
        return pltpu.make_async_remote_copy(
            src_ref=src,
            dst_ref=dst,
            send_sem=send,
            recv_sem=recv,
            device_id=target,
            device_id_type=MESH,
        )

    halo_copies = []
    for k, offset in enumerate(OFFSETS):
        back_slot = len(OFFSETS) - 1 - k
        halo_copies.append(remote(
            stage.at[k], arrived.at[back_slot], halo_send.at[k], halo_recv.at[back_slot],
            (me + offset, rank),
        ))
    for k in sorted(range(len(OFFSETS)), key=lambda i: -abs(OFFSETS[i])):
        target = me + OFFSETS[k]

        @pl.when((target >= 0) & (target < devices))
        def _(copy=halo_copies[k]):
            copy.start()

    def gather(piece, send, recv):
        here = piece(rank)
        direct = [remote(here, here, send.at[0], recv.at[0], (me, pair))]
        passed = []
        for j in range(1, half_ranks):
            ahead = lax.rem(rank + CORES * j, ranks)
            behind = piece(lax.rem(rank + ranks - CORES * j, ranks))
            direct.append(remote(here, here, send.at[j], recv.at[j], (me, ahead)))
            k = half_ranks + j - 1
            passed.append(remote(behind, behind, send.at[k], recv.at[k], (me, pair)))
        return direct, passed

    def start(copies):
        for copy in copies:
            copy.start()

    def arrive(copies):
        for copy in copies:
            copy.wait_recv()

    own_rows = pl.ds(0, LIVE_MAX)
    own_copies, own_passed = gather(lambda r: table.at[own_rows, r], own_send, own_recv)
    start(own_copies[::-1])

    loads["back"].wait()
    loads["old"].wait()
    old_start, old_end = old_ref[me], old_ref[me + 1]
    back_all = back_ref[...].astype(F32)
    for s in range(capacity):
        back_t[s] = back_all[:, s, :].astype(BF16)
    old_count = old_end - old_start
    for c in range(MOVE):
        mig_out[0, c] = back_t[jnp.clip(c, 0, capacity - 1)]
        mig_out[1, c] = back_t[jnp.clip(old_count - MOVE + c, 0, capacity - 1)]
    mig_copies = []
    for side, offset in ((0, -1), (1, 1)):
        target = me + offset
        copy = remote(
            mig_out.at[side], mig_in.at[1 - side], mig_send.at[side], mig_recv.at[1 - side],
            (target, rank),
        )
        mig_copies.append(copy)

        @pl.when((target >= 0) & (target < devices))
        def _(copy=copy):
            copy.start()

    early = range(MOVE, TILE_MEAN - 2 * MOVE)
    for s in early:
        states[s, rank, :members] = back_t[jnp.clip(new_start + s - old_start, 0, capacity - 1)]
    early_rows = pl.ds(early.start, len(early))
    early_copies, early_passed = gather(lambda r: states.at[early_rows, r], early_send, early_recv)
    start(early_copies[::-1])

    arrive(own_copies[1:])
    start(own_passed)

    for k, offset in enumerate(OFFSETS):
        back_slot = len(OFFSETS) - 1 - k
        source = me + OFFSETS[back_slot]

        @pl.when((source >= 0) & (source < devices))
        def _(copy=halo_copies[k]):
            copy.wait_recv()

    far = []
    for g in range(HPEER):
        first = halo_ref[me, g * HCAP]
        owner = jnp.int32(0)
        for k, offset in enumerate(OFFSETS):
            source = jnp.clip(me + offset, 0, devices - 1)
            held = (first >= new_ref[source]) & (first < new_ref[source + 1])
            inside = (me + offset >= 0) & (me + offset < devices)
            owner = jnp.where(held & inside, k, owner)
        for c in range(HCAP):
            table[LIVE_MAX + g * HCAP + c, rank] = arrived[owner, c]
        rows = pl.ds(LIVE_MAX + g * HCAP, HCAP)
        far.append(gather(lambda r, rows=rows: table.at[rows, r], far_send.at[g], far_recv.at[g]))
        start(far[g][0][::-1])

    for side, offset in ((0, -1), (1, 1)):
        source = me - offset

        @pl.when((source >= 0) & (source < devices))
        def _(copy=mig_copies[side]):
            copy.wait_recv()

    late = []
    for first, last in ((early.stop, LIVE_MAX), (0, early.start)):
        for s in range(first, last):
            position = new_start + s
            left = mig_in[0, jnp.clip(position - old_start + MOVE, 0, MOVE - 1)]
            own = back_t[jnp.clip(position - old_start, 0, capacity - 1)]
            right = mig_in[1, jnp.clip(position - old_end, 0, MOVE - 1)]
            row = jnp.where(position < old_start, left, jnp.where(position < old_end, own, right))
            states[s, rank, :members] = row
        rows = pl.ds(first, last - first)
        k = len(late)
        late.append(gather(lambda r, rows=rows: states.at[rows, r], state_send.at[k], state_recv.at[k]))
        start(late[k][0][::-1])

    arrive(early_copies[1:])
    start(early_passed)
    arrive(own_copies[:1] + own_passed)

    blank = jnp.zeros((LANES - full, obs_slots), BF16)

    def product(index):
        block = table[index].reshape(full, obs_slots)
        wide = jnp.concatenate([block, blank], axis=0)
        gram_s[index] = lax.dot_general(
            block, wide, (((1,), (1,)), ((), ())), preferred_element_type=F32
        )

    for s in range(LIVE_MAX):
        product(s)

    for g in range(HPEER):
        arrive(far[g][0][1:])
        start(far[g][1])
    for g in range(HPEER):
        arrive(far[g][0][:1] + far[g][1])
        for c in range(HCAP):
            product(LIVE_MAX + g * HCAP + c)

    shape = (full, LANES)
    grid_row = lax.broadcasted_iota(jnp.int32, shape, 0)
    grid_col = lax.broadcasted_iota(jnp.int32, shape, 1)
    live_row = lax.rem(grid_row, PAD) < members
    live_col = (lax.rem(grid_col, PAD) < members) & (grid_col < full)
    rider = grid_row == members
    live = live_row & live_col
    kept = (live_row | rider) & live_col
    unit = jnp.where(live & (grid_row == grid_col), 1.0, 0.0)
    half_unit = 1.5 * unit
    shift = (ensemble - 1) / INFLATION
    loads["region"].wait()
    loads["weight"].wait()
    entries = region_ref.shape[0]
    fill = jnp.zeros((LANES - full, LANES), BF16)

    def tall(a):
        return jnp.concatenate([a, fill], axis=0)

    def times(left, high, low):
        both = jnp.concatenate([high, high], axis=0)
        return dot(left, both) + dot(left[:, :LANES], low)

    def wide(a):
        high, low = cut(a)
        return jnp.concatenate([high, low], axis=1)

    norms = []
    for b in range(per_core):
        slot = jnp.minimum(CORES * b + core, LIVE_MAX - 1)
        gram = gram_s[slot]
        for e in range(entries):
            named = region_ref[e, slot]
            index = jnp.where(named < capacity, named, named - capacity + LIVE_MAX)
            index = jnp.clip(index, 0, LIVE_MAX + halo_count - 1)
            gram += weight_ref[e, slot] * gram_s[index]
        system = jnp.where(kept, gram, 0.0) + shift * unit
        square = jnp.where(live, system * system, 0.0)
        total = jnp.sum(jnp.sum(square, axis=1, keepdims=True), axis=0, keepdims=True)
        norm = jnp.sqrt(total)
        norms.append(norm)
        y = system / norm
        middle = half_unit - 0.5 * jnp.where(live, y, 0.0)
        high, low = cut(middle)
        first = times(wide(y), tall(high), tall(low))
        yz_s[b, :full] = wide(jnp.where(rider, 0.0, first))
        yz_s[b, full : 2 * full] = wide(jnp.where(rider, first, middle))

    def cross(b):
        z = yz_s[b, full : 2 * full]
        return times(z, yz_s[b, :LANES, :LANES], yz_s[b, :LANES, LANES:])

    def step(_, carry):
        middles = []
        for b in range(per_core):
            high, low = cut(half_unit - 0.5 * cross(b))
            middles.append((tall(high), tall(low)))
        for b in range(per_core):
            yz_s[b, : 2 * full] = wide(times(yz_s[b, : 2 * full], *middles[b]))
        return carry

    lax.fori_loop(0, NS_ITERS - 2, step, 0)

    piece = CORES * PAD
    block = 16
    start_row = members // block * block
    middles, riders = [], []
    for b in range(per_core):
        high, low = cut(half_unit - 0.5 * cross(b))
        middles.append((tall(high), tall(low)))
        q = yz_s[b, full + start_row : full + start_row + block]
        z_rows = slice(full, full + LANES)
        riders.append(times(q, yz_s[b, z_rows, :LANES], yz_s[b, z_rows, LANES:]))
    for b in range(per_core):
        chosen = yz_s[b, pl.ds(pl.multiple_of(full + chip * piece, block), piece)]
        stack = jnp.concatenate([chosen, wide(riders[b])], axis=0)
        both = times(stack, *middles[b])
        lead = times(wide(both[piece:]), *middles[b])[members - start_row : members - start_row + 1]
        spread = math.sqrt(ensemble - 1) * lax.rsqrt(norms[b])
        t_full[:, b] = (spread * both[:piece] + lead).astype(BF16).reshape(CORES, PAD, LANES)

    other = 1 - core
    t_copy = remote(t_full.at[other], t_all.at[core], t_send, t_recv, (me, pair))
    t_copy.start()
    t_all[core] = t_full[core]

    for direct, passed in late:
        arrive(direct[1:])
        start(passed)
    arrive(early_copies[:1] + early_passed)
    for direct, passed in late:
        arrive(direct[:1] + passed)
    t_copy.wait_recv()

    piece_row = lax.broadcasted_iota(jnp.int32, (PAD, full), 0)
    for s in range(LIVE_MAX):
        weights = t_all[s % CORES, s // CORES][:, :full]
        weights = jnp.where(piece_row == members, jnp.ones_like(weights), weights)
        keep = 1.0 - jnp.sum(weights.astype(F32), axis=1, keepdims=True)
        blended = dot(weights, states[s].reshape(full, width))
        mean = blended[members : members + 1, :] / ensemble
        value = (blended + keep * mean)[:members]
        is_live = new_start + s < new_end
        out_ref[s] = jnp.where(is_live, value, 0.0).astype(BF16)
    for s in range(LIVE_MAX, capacity):
        out_ref[s] = jnp.zeros((members, width), BF16)

    for k, offset in enumerate(OFFSETS):
        target = me + offset

        @pl.when((target >= 0) & (target < devices))
        def _(copy=halo_copies[k]):
            copy.wait_send()

    for side, offset in ((0, -1), (1, 1)):
        target = me + offset

        @pl.when((target >= 0) & (target < devices))
        def _(copy=mig_copies[side]):
            copy.wait_send()

    gathers = own_copies + own_passed + early_copies + early_passed + [t_copy]
    for direct, passed in far + late:
        gathers += direct + passed
    for copy in gathers:
        copy.wait_send()


def shards(devices, ranks, background, obs_ens, innovation, precision, loc_weight, old_split,
           new_split, obs_count, halo_tiles, region_list):
    capacity, members, width = background.shape
    obs_slots = obs_ens.shape[2]
    full = PAD * ranks
    halo_count = HPEER * HCAP
    per_core = -(-LIVE_MAX // CORES)
    hbm = pl.BlockSpec(memory_space=pltpu.MemorySpace.HBM)
    vmem = pl.BlockSpec(memory_space=pltpu.VMEM)
    count = len(OFFSETS)
    dma = pltpu.SemaphoreType.DMA
    operands = (old_split, new_split, obs_count, halo_tiles, region_list.T, loc_weight.T,
                jnp.swapaxes(background, 0, 1), jnp.swapaxes(obs_ens, 0, 1), innovation, precision)
    spaces = [pltpu.SMEM] * 6 + [pltpu.VMEM] * 4
    return pl.pallas_call(
        functools.partial(kernel, devices, ranks),
        out_shape=pltpu.VMEM((capacity, members, width), BF16),
        in_specs=[hbm] * len(operands),
        out_specs=vmem,
        scratch_shapes=[space(x.shape, x.dtype) for space, x in zip(spaces, operands)] + [
            pltpu.VMEM((LIVE_MAX, PAD, obs_slots), BF16),
            pltpu.VMEM((capacity, members, width), BF16),
            pltpu.VMEM((LIVE_MAX + halo_count, ranks, PAD, obs_slots), BF16),
            pltpu.VMEM((count, HCAP, PAD, obs_slots), BF16),
            pltpu.VMEM((count, HCAP, PAD, obs_slots), BF16),
            pltpu.VMEM((2, MOVE, members, width), BF16),
            pltpu.VMEM((2, MOVE, members, width), BF16),
            pltpu.VMEM((LIVE_MAX, ranks, PAD, width), BF16),
            pltpu.VMEM((LIVE_MAX + halo_count, full, LANES), F32),
            pltpu.VMEM((per_core, full + LANES, 2 * LANES), BF16),
            pltpu.VMEM((CORES, per_core, PAD, LANES), BF16),
            pltpu.VMEM((CORES, per_core, PAD, LANES), BF16),
            dma((len(operands),)),
            dma((count,)),
            dma((count,)),
            dma((2,)),
            dma((2,)),
            dma((ranks - 1,)),
            dma((ranks - 1,)),
            dma((HPEER, ranks - 1)),
            dma((HPEER, ranks - 1)),
            dma((ranks - 1,)),
            dma((ranks - 1,)),
            dma((2, ranks - 1)),
            dma((2, ranks - 1)),
            dma,
            dma,
        ],
        compiler_params=pltpu.CompilerParams(
            collective_id=0, has_side_effects=True
        ),
        cost_estimate=pl.CostEstimate(flops=10**8, bytes_accessed=10**7, transcendentals=0),
    )(*operands)


def solution(mesh):
    in_specs = (
        P("tile", "mem", None),
        P("tile", "mem", None),
        P("tile", None),
        P("tile", None),
        P("tile", None),
        P(),
        P(),
        P("tile"),
        P(),
        P("tile", None),
    )
    out_specs = P("tile", "mem", None)
    body = functools.partial(shards, mesh.shape["tile"], mesh.shape["mem"])
    return jax.shard_map(body, mesh=mesh, in_specs=in_specs, out_specs=out_specs, check_vma=False)
```

time: 24.6 us -> 21 us (0.85)
  Pallas kernels: 22.6 us -> 20 us
  local copies, waits for them, and re-layouts: 1.79 us -> 0.82 us
    pallas_call x1, Pallas kernels: 22.6 us -> 20 us  [shards(): pl.pallas_call(functools.partial(kernel, devices, ranks), out_shape=pltpu...]
    pallas_call x1, local copies, waits for them, and re-layouts: 1.79 us -> 0.82 us  [shards(): pl.pallas_call(functools.partial(kernel, devices, ranks), out_shape=pltpu...]
where the time goes in v1:
time: 21 us; the launch traced here: 20.9 us
  Pallas kernels  20 us (95%)
  local copies, waits for them, and re-layouts  0.82 us (4%)
    pallas_call x1, Pallas kernels, shards(): pl.pallas_call(functools.partial(kernel, devices, ranks), out_shape=pltpu...  20 us
    pallas_call x1, local copies, waits for them, and re-layouts, shards(): pl.pallas_call(functools.partial(kernel, devices, ranks), out_shape=pltpu...  0.82 us

profile of v1, /device:TPU:0, one launch (start us, length us, event | category | flops | bytes accessed | tf_op | source)
XLA Modules:
  0.0 20.9 jit_solution(7989708191589354303)
XLA Ops:
  0.0 20.0 %shard_map.100 = bf16[14,20,512]{2,1,0:T(8,128)(2,1)S(1)} custom-call(s32[9]{0:T(128)} %old_hbm.1, s32[9]{0:T(128)} %new_hbm.1, s32[14]{0:T(128)} %count_hbm.1, s32[8,12]{1,0:T(8,128)} %halo_hbm.1, s32[7,14]{1,0:T(8,128)} %bitcast.6, f32[7,14]{1,0:T(8,128)} %bitcast.7, bf16[20,14,512]{2,1,0:T(8,128)(2,1)} %bitcast.4, bf16[20,14,128]{2,1,0:T(8,128)(2,1)} %bitcast.5, ...), custom_call_target="tpu_custom_call" | custom-call | flops 100000000 | bytes 10000000 | tf_op jit(solution)/shard_map/pallas_call | solution.py:463
  20.0 0.8 %copy.11 = bf16[14,20,512]{2,0,1:T(8,128)(2,1)} copy(bf16[14,20,512]{2,1,0:T(8,128)(2,1)S(1)} %shard_map.100) | data formatting | bytes 573440 | tf_op jit(solution)/shard_map/pallas_call | solution.py:463

commit v2 on v1

--- a/solution.py
+++ b/solution.py
@@ -71,16 +71,11 @@
     t_full,
     t_all,
     load_sem,
-    halo_send,
     halo_recv,
-    mig_send,
     mig_recv,
-    own_send,
     own_recv,
     far_send,
     far_recv,
-    early_send,
-    early_recv,
     state_send,
     state_recv,
     t_send,
@@ -98,18 +93,19 @@
     chip = rank // CORES
     pair = rank + 1 - 2 * core
     half_ranks = ranks // CORES
-    peers = [lax.rem(rank + j, ranks) for j in range(1, ranks)]
+
+    def signal(sem, tile, to):
+        pl.semaphore_signal(sem, inc=1, device_id=(tile, to), device_id_type=MESH)
 
     barrier = pltpu.get_barrier_semaphore()
     for offset in OFFSETS:
-        target = me + offset
-
-        @pl.when((target >= 0) & (target < devices))
-        def _():
-            pl.semaphore_signal(barrier, inc=1, device_id=(target, rank), device_id_type=MESH)
-
-    for peer in peers:
-        pl.semaphore_signal(barrier, inc=1, device_id=(me, peer), device_id_type=MESH)
+
+        @pl.when((me + offset >= 0) & (me + offset < devices))
+        def _(offset=offset):
+            signal(barrier, me + offset, rank)
+
+    for j in range(1, ranks):
+        signal(barrier, me, lax.rem(rank + j, ranks))
 
     loads = {}
     for k, (name, src, dst) in enumerate((
@@ -151,24 +147,8 @@
 
     loads["new"].wait()
     loads["halo"].wait()
+    loads["region"].wait()
     new_start, new_end = new_ref[me], new_ref[me + 1]
-    for k, offset in enumerate(OFFSETS):
-        reader = jnp.clip(me + offset, 0, devices - 1)
-        for c in range(HCAP):
-            index = jnp.int32(0)
-            for g in range(HPEER):
-                first = halo_ref[reader, g * HCAP]
-                here = (first >= new_start) & (first < new_end)
-                index += jnp.where(here, halo_ref[reader, g * HCAP + c] - new_start, 0)
-            index = jnp.clip(index, 0, LIVE_MAX - 1)
-            stage[k, c] = mine[index]
-
-    signals = ranks - 1
-    for offset in OFFSETS:
-        inside = (me + offset >= 0) & (me + offset < devices)
-        signals += jnp.where(inside, 1, 0)
-    pl.semaphore_wait(barrier, signals)
-
     def remote(src, dst, send, recv, target):
         return pltpu.make_async_remote_copy(
             src_ref=src,
@@ -179,46 +159,63 @@
             device_id_type=MESH,
         )
 
+    def fill_stage(k):
+        reader = jnp.clip(me + OFFSETS[k], 0, devices - 1)
+        for c in range(HCAP):
+            index = jnp.int32(0)
+            for g in range(HPEER):
+                first = halo_ref[reader, g * HCAP]
+                here = (first >= new_start) & (first < new_end)
+                index += jnp.where(here, halo_ref[reader, g * HCAP + c] - new_start, 0)
+            index = jnp.clip(index, 0, LIVE_MAX - 1)
+            stage[k, c] = mine[index]
+
     halo_copies = []
     for k, offset in enumerate(OFFSETS):
         back_slot = len(OFFSETS) - 1 - k
         halo_copies.append(remote(
-            stage.at[k], arrived.at[back_slot], halo_send.at[k], halo_recv.at[back_slot],
+            stage.at[k], arrived.at[back_slot], load_sem.at[k], halo_recv.at[back_slot],
             (me + offset, rank),
         ))
+    for k in range(len(OFFSETS)):
+        fill_stage(k)
+    pl.semaphore_wait(barrier, jnp.minimum(me, REACH) + jnp.minimum(devices - 1 - me, REACH) + ranks - 1)
     for k in sorted(range(len(OFFSETS)), key=lambda i: -abs(OFFSETS[i])):
-        target = me + OFFSETS[k]
-
-        @pl.when((target >= 0) & (target < devices))
+
+        @pl.when((me + OFFSETS[k] >= 0) & (me + OFFSETS[k] < devices))
         def _(copy=halo_copies[k]):
             copy.start()
 
-    def gather(piece, send, recv):
+    def send_own(piece, send, ahead_recv, pair_recv):
         here = piece(rank)
-        direct = [remote(here, here, send.at[0], recv.at[0], (me, pair))]
-        passed = []
         for j in range(1, half_ranks):
             ahead = lax.rem(rank + CORES * j, ranks)
+            remote(here, here, send, ahead_recv, (me, ahead)).start()
+        remote(here, here, send, pair_recv, (me, pair)).start()
+
+    def send_passed(piece, send, pair_recv):
+        for j in range(1, half_ranks):
             behind = piece(lax.rem(rank + ranks - CORES * j, ranks))
-            direct.append(remote(here, here, send.at[j], recv.at[j], (me, ahead)))
-            k = half_ranks + j - 1
-            passed.append(remote(behind, behind, send.at[k], recv.at[k], (me, pair)))
-        return direct, passed
-
-    def start(copies):
-        for copy in copies:
-            copy.start()
-
-    def arrive(copies):
-        for copy in copies:
-            copy.wait_recv()
-
-    own_rows = pl.ds(0, LIVE_MAX)
-    own_copies, own_passed = gather(lambda r: table.at[own_rows, r], own_send, own_recv)
-    start(own_copies[::-1])
+            remote(behind, behind, send, pair_recv, (me, pair)).start()
+
+    def whole_of(piece, sem, count):
+        block = piece(pl.ds(0, count))
+        return pltpu.make_async_copy(block, block, sem)
+
+    def arrive_ahead(piece, sem):
+        whole_of(piece, sem, half_ranks - 1).wait()
+
+    def arrive_pair(piece, sem):
+        whole_of(piece, sem, half_ranks).wait()
+
+    def own_piece(r):
+        return table.at[0:LIVE_MAX, r]
+
+    send_own(own_piece, load_sem.at[8], own_recv.at[0], own_recv.at[1])
 
     loads["back"].wait()
     loads["old"].wait()
+    loads["weight"].wait()
     old_start, old_end = old_ref[me], old_ref[me + 1]
     back_all = back_ref[...].astype(F32)
     for s in range(capacity):
@@ -231,24 +228,36 @@
     for side, offset in ((0, -1), (1, 1)):
         target = me + offset
         copy = remote(
-            mig_out.at[side], mig_in.at[1 - side], mig_send.at[side], mig_recv.at[1 - side],
+            mig_out.at[side], mig_in.at[1 - side], load_sem.at[len(OFFSETS) + side], mig_recv.at[1 - side],
             (target, rank),
         )
         mig_copies.append(copy)
 
-        @pl.when((target >= 0) & (target < devices))
-        def _(copy=copy):
-            copy.start()
+    @pl.when(me > 0)
+    def _():
+        mig_copies[0].start()
 
     early = range(MOVE, TILE_MEAN - 2 * MOVE)
     for s in early:
         states[s, rank, :members] = back_t[jnp.clip(new_start + s - old_start, 0, capacity - 1)]
-    early_rows = pl.ds(early.start, len(early))
-    early_copies, early_passed = gather(lambda r: states.at[early_rows, r], early_send, early_recv)
-    start(early_copies[::-1])
-
-    arrive(own_copies[1:])
-    start(own_passed)
+
+    def early_piece(r):
+        return states.at[early.start : early.stop, r]
+
+    def first_piece(r):
+        return states.at[0 : early.start, r]
+
+    def last_piece(r):
+        return states.at[early.stop : LIVE_MAX, r]
+
+    def every_piece(r):
+        return states.at[0:LIVE_MAX, r]
+
+    send_own(early_piece, state_send, state_recv.at[0], state_recv.at[1])
+
+    @pl.when(me + 1 < devices)
+    def _():
+        mig_copies[1].start()
 
     for k, offset in enumerate(OFFSETS):
         back_slot = len(OFFSETS) - 1 - k
@@ -269,34 +278,17 @@
             owner = jnp.where(held & inside, k, owner)
         for c in range(HCAP):
             table[LIVE_MAX + g * HCAP + c, rank] = arrived[owner, c]
-        rows = pl.ds(LIVE_MAX + g * HCAP, HCAP)
-        far.append(gather(lambda r, rows=rows: table.at[rows, r], far_send.at[g], far_recv.at[g]))
-        start(far[g][0][::-1])
-
-    for side, offset in ((0, -1), (1, 1)):
-        source = me - offset
-
-        @pl.when((source >= 0) & (source < devices))
-        def _(copy=mig_copies[side]):
-            copy.wait_recv()
-
-    late = []
-    for first, last in ((early.stop, LIVE_MAX), (0, early.start)):
-        for s in range(first, last):
-            position = new_start + s
-            left = mig_in[0, jnp.clip(position - old_start + MOVE, 0, MOVE - 1)]
-            own = back_t[jnp.clip(position - old_start, 0, capacity - 1)]
-            right = mig_in[1, jnp.clip(position - old_end, 0, MOVE - 1)]
-            row = jnp.where(position < old_start, left, jnp.where(position < old_end, own, right))
-            states[s, rank, :members] = row
-        rows = pl.ds(first, last - first)
-        k = len(late)
-        late.append(gather(lambda r, rows=rows: states.at[rows, r], state_send.at[k], state_recv.at[k]))
-        start(late[k][0][::-1])
-
-    arrive(early_copies[1:])
-    start(early_passed)
-    arrive(own_copies[:1] + own_passed)
+        first_row = LIVE_MAX + g * HCAP
+
+        def far_piece(r, first_row=first_row):
+            return table.at[first_row : first_row + HCAP, r]
+
+        far.append(far_piece)
+        send_own(far_piece, far_send.at[g], far_recv.at[0, g], far_recv.at[1, g])
+
+    arrive_ahead(own_piece, own_recv.at[0])
+    send_passed(own_piece, load_sem.at[8], own_recv.at[1])
+    arrive_pair(own_piece, own_recv.at[1])
 
     blank = jnp.zeros((LANES - full, obs_slots), BF16)
 
@@ -310,13 +302,44 @@
     for s in range(LIVE_MAX):
         product(s)
 
-    for g in range(HPEER):
-        arrive(far[g][0][1:])
-        start(far[g][1])
-    for g in range(HPEER):
-        arrive(far[g][0][:1] + far[g][1])
+    for side, offset in ((0, -1), (1, 1)):
+        source = me - offset
+
+        @pl.when((source >= 0) & (source < devices))
+        def _(copy=mig_copies[side]):
+            copy.wait_recv()
+
+    for s in [*range(early.stop, LIVE_MAX), *range(early.start)]:
+        position = new_start + s
+        left = mig_in[0, jnp.clip(position - old_start + MOVE, 0, MOVE - 1)]
+        own = back_t[jnp.clip(position - old_start, 0, capacity - 1)]
+        right = mig_in[1, jnp.clip(position - old_end, 0, MOVE - 1)]
+        row = jnp.where(position < old_start, left, jnp.where(position < old_end, own, right))
+        states[s, rank, :members] = row
+    for piece in (last_piece, first_piece):
+        send_own(piece, state_send, state_recv.at[0], state_recv.at[1])
+
+    def pass_far(g):
+        arrive_ahead(far[g], far_recv.at[0, g])
+        send_passed(far[g], far_send.at[g], far_recv.at[1, g])
+
+    def far_products(g):
+        arrive_pair(far[g], far_recv.at[1, g])
         for c in range(HCAP):
             product(LIVE_MAX + g * HCAP + c)
+
+    @pl.when(core == 0)
+    def _():
+        for g in range(HPEER):
+            pass_far(g)
+            far_products(g)
+
+    @pl.when(core != 0)
+    def _():
+        for g in range(HPEER):
+            pass_far(g)
+        for g in range(HPEER):
+            far_products(g)
 
     shape = (full, LANES)
     grid_row = lax.broadcasted_iota(jnp.int32, shape, 0)
@@ -329,8 +352,6 @@
     unit = jnp.where(live & (grid_row == grid_col), 1.0, 0.0)
     half_unit = 1.5 * unit
     shift = (ensemble - 1) / INFLATION
-    loads["region"].wait()
-    loads["weight"].wait()
     entries = region_ref.shape[0]
     fill = jnp.zeros((LANES - full, LANES), BF16)
 
@@ -379,7 +400,8 @@
             yz_s[b, : 2 * full] = wide(times(yz_s[b, : 2 * full], *middles[b]))
         return carry
 
-    lax.fori_loop(0, NS_ITERS - 2, step, 0)
+    for k in range(NS_ITERS - 2):
+        step(k, 0)
 
     piece = CORES * PAD
     block = 16
@@ -404,15 +426,12 @@
     t_copy.start()
     t_all[core] = t_full[core]
 
-    for direct, passed in late:
-        arrive(direct[1:])
-        start(passed)
-    arrive(early_copies[:1] + early_passed)
-    for direct, passed in late:
-        arrive(direct[:1] + passed)
+    arrive_ahead(every_piece, state_recv.at[0])
+    send_passed(every_piece, state_send, state_recv.at[1])
+    arrive_pair(every_piece, state_recv.at[1])
+
+    piece_row = lax.broadcasted_iota(jnp.int32, (PAD, full), 0)
     t_copy.wait_recv()
-
-    piece_row = lax.broadcasted_iota(jnp.int32, (PAD, full), 0)
     for s in range(LIVE_MAX):
         weights = t_all[s % CORES, s // CORES][:, :full]
         weights = jnp.where(piece_row == members, jnp.ones_like(weights), weights)
@@ -439,11 +458,11 @@
         def _(copy=mig_copies[side]):
             copy.wait_send()
 
-    gathers = own_copies + own_passed + early_copies + early_passed + [t_copy]
-    for direct, passed in far + late:
-        gathers += direct + passed
-    for copy in gathers:
-        copy.wait_send()
+    t_copy.wait_send()
+    whole_of(own_piece, load_sem.at[8], ranks - 1).wait()
+    whole_of(every_piece, state_send, ranks - 1).wait()
+    for g in range(HPEER):
+        whole_of(far[g], far_send.at[g], ranks - 1).wait()
 
 
 def shards(devices, ranks, background, obs_ens, innovation, precision, loc_weight, old_split,
@@ -480,17 +499,12 @@
             pltpu.VMEM((CORES, per_core, PAD, LANES), BF16),
             dma((len(operands),)),
             dma((count,)),
-            dma((count,)),
             dma((2,)),
             dma((2,)),
-            dma((ranks - 1,)),
-            dma((ranks - 1,)),
-            dma((HPEER, ranks - 1)),
-            dma((HPEER, ranks - 1)),
-            dma((ranks - 1,)),
-            dma((ranks - 1,)),
-            dma((2, ranks - 1)),
-            dma((2, ranks - 1)),
+            dma((HPEER,)),
+            dma((2, HPEER)),
+            dma,
+            dma((2,)),
             dma,
             dma,
         ],

time: 21 us -> 19.4 us (0.924)
  Pallas kernels: 20 us -> 18.4 us
    pallas_call x1, Pallas kernels: 20 us -> 18.4 us  [shards(): pl.pallas_call(functools.partial(kernel, devices, ranks), out_shape=pltpu...]
where the time goes in v2:
time: 19.4 us; the launch traced here: 19.3 us
  Pallas kernels  18.4 us (95%)
  local copies, waits for them, and re-layouts  0.82 us (4%)
    pallas_call x1, Pallas kernels, shards(): pl.pallas_call(functools.partial(kernel, devices, ranks), out_shape=pltpu...  18.4 us
    pallas_call x1, local copies, waits for them, and re-layouts, shards(): pl.pallas_call(functools.partial(kernel, devices, ranks), out_shape=pltpu...  0.82 us

profile of v2, /device:TPU:0, one launch (start us, length us, event | category | flops | bytes accessed | tf_op | source)
XLA Modules:
  0.0 19.3 jit_solution(12044085936693577601)
XLA Ops:
  0.0 18.4 %shard_map.100 = bf16[14,20,512]{2,1,0:T(8,128)(2,1)S(1)} custom-call(s32[9]{0:T(128)} %old_hbm.1, s32[9]{0:T(128)} %new_hbm.1, s32[14]{0:T(128)} %count_hbm.1, s32[8,12]{1,0:T(8,128)} %halo_hbm.1, s32[7,14]{1,0:T(8,128)} %bitcast.6, f32[7,14]{1,0:T(8,128)} %bitcast.7, bf16[20,14,512]{2,1,0:T(8,128)(2,1)} %bitcast.4, bf16[20,14,128]{2,1,0:T(8,128)(2,1)} %bitcast.5, ...), custom_call_target="tpu_custom_call" | custom-call | flops 100000000 | bytes 10000000 | tf_op jit(solution)/shard_map/pallas_call | solution.py:482
  18.5 0.8 %copy.11 = bf16[14,20,512]{2,0,1:T(8,128)(2,1)} copy(bf16[14,20,512]{2,1,0:T(8,128)(2,1)S(1)} %shard_map.100) | data formatting | bytes 573440 | tf_op jit(solution)/shard_map/pallas_call | solution.py:482

commit v3 on v2

--- a/solution.py
+++ b/solution.py
@@ -70,6 +70,7 @@
     yz_s,
     t_full,
     t_all,
+    right_sem,
     load_sem,
     halo_recv,
     mig_recv,
@@ -98,9 +99,9 @@
         pl.semaphore_signal(sem, inc=1, device_id=(tile, to), device_id_type=MESH)
 
     barrier = pltpu.get_barrier_semaphore()
-    for offset in OFFSETS:
-
-        @pl.when((me + offset >= 0) & (me + offset < devices))
+    for offset in range(1, REACH + 1):
+
+        @pl.when(me + offset < devices)
         def _(offset=offset):
             signal(barrier, me + offset, rank)
 
@@ -123,6 +124,13 @@
         loads[name] = pltpu.make_async_copy(src, dst, load_sem.at[k])
         loads[name].start()
 
+    pl.semaphore_wait(barrier, jnp.minimum(me, REACH) + ranks - 1)
+    for offset in range(1, REACH + 1):
+
+        @pl.when(me - offset >= 0)
+        def _(offset=offset):
+            signal(right_sem.at[offset - 1], me - offset, rank)
+
     row_id = lax.broadcasted_iota(jnp.int32, (PAD, obs_slots), 0)
     lane_id = lax.broadcasted_iota(jnp.int32, (1, obs_slots), 1)
 
@@ -177,14 +185,15 @@
             stage.at[k], arrived.at[back_slot], load_sem.at[k], halo_recv.at[back_slot],
             (me + offset, rank),
         ))
-    for k in range(len(OFFSETS)):
+    for k in range(REACH):
         fill_stage(k)
-    pl.semaphore_wait(barrier, jnp.minimum(me, REACH) + jnp.minimum(devices - 1 - me, REACH) + ranks - 1)
-    for k in sorted(range(len(OFFSETS)), key=lambda i: -abs(OFFSETS[i])):
-
-        @pl.when((me + OFFSETS[k] >= 0) & (me + OFFSETS[k] < devices))
+
+        @pl.when(me + OFFSETS[k] >= 0)
         def _(copy=halo_copies[k]):
             copy.start()
+
+    for k in range(REACH, len(OFFSETS)):
+        fill_stage(k)
 
     def send_own(piece, send, ahead_recv, pair_recv):
         here = piece(rank)
@@ -255,9 +264,15 @@
 
     send_own(early_piece, state_send, state_recv.at[0], state_recv.at[1])
 
-    @pl.when(me + 1 < devices)
-    def _():
-        mig_copies[1].start()
+    for offset in range(1, REACH + 1):
+
+        @pl.when(me + offset < devices)
+        def _(offset=offset):
+            pl.semaphore_wait(right_sem.at[offset - 1], 1)
+            halo_copies[OFFSETS.index(offset)].start()
+            if offset == 1:
+                mig_copies[1].start()
+
 
     for k, offset in enumerate(OFFSETS):
         back_slot = len(OFFSETS) - 1 - k
@@ -497,6 +512,7 @@
             pltpu.VMEM((per_core, full + LANES, 2 * LANES), BF16),
             pltpu.VMEM((CORES, per_core, PAD, LANES), BF16),
             pltpu.VMEM((CORES, per_core, PAD, LANES), BF16),
+            pltpu.SemaphoreType.REGULAR((REACH,)),
             dma((len(operands),)),
             dma((count,)),
             dma((2,)),

time: 19.4 us -> 18.6 us (0.959)
  the two profiles are of different devices: /device:TPU:0 before, /device:TPU:25 now
where the time goes in v3:
time: 18.6 us; the launch traced here: 18.5 us
  Pallas kernels  17.6 us (95%)
  local copies, waits for them, and re-layouts  0.82 us (4%)
    pallas_call x1, Pallas kernels, shards(): pl.pallas_call(functools.partial(kernel, devices, ranks), out_shape=pltpu...  17.6 us
    pallas_call x1, local copies, waits for them, and re-layouts, shards(): pl.pallas_call(functools.partial(kernel, devices, ranks), out_shape=pltpu...  0.82 us

profile of v3, /device:TPU:25, one launch (start us, length us, event | category | flops | bytes accessed | tf_op | source)
XLA Modules:
  0.0 18.5 jit_solution(10707055571436167422)
XLA Ops:
  0.0 17.6 %shard_map.100 = bf16[14,20,512]{2,1,0:T(8,128)(2,1)S(1)} custom-call(s32[9]{0:T(128)} %old_hbm.1, s32[9]{0:T(128)} %new_hbm.1, s32[14]{0:T(128)} %count_hbm.1, s32[8,12]{1,0:T(8,128)} %halo_hbm.1, s32[7,14]{1,0:T(8,128)} %bitcast.6, f32[7,14]{1,0:T(8,128)} %bitcast.7, bf16[20,14,512]{2,1,0:T(8,128)(2,1)} %bitcast.4, bf16[20,14,128]{2,1,0:T(8,128)(2,1)} %bitcast.5, ...), custom_call_target="tpu_custom_call" | custom-call | flops 100000000 | bytes 10000000 | tf_op jit(solution)/shard_map/pallas_call | solution.py:497
  17.6 0.8 %copy.11 = bf16[14,20,512]{2,0,1:T(8,128)(2,1)} copy(bf16[14,20,512]{2,1,0:T(8,128)(2,1)S(1)} %shard_map.100) | data formatting | bytes 573440 | tf_op jit(solution)/shard_map/pallas_call | solution.py:497

commit v4 on v3

--- a/solution.py
+++ b/solution.py
@@ -22,6 +22,7 @@
 F32 = jnp.float32
 BF16 = jnp.bfloat16
 LANES = 128
+SPLIT = 6
 OFFSETS = tuple(range(-REACH, 0)) + tuple(range(1, REACH + 1))
 
 
@@ -87,7 +88,7 @@
     ensemble = members * ranks
     full = PAD * ranks
     halo_count = HPEER * HCAP
-    per_core = -(-LIVE_MAX // CORES)
+    per_core = max(SPLIT, LIVE_MAX - SPLIT)
     me = lax.axis_index("tile")
     rank = lax.axis_index("mem")
     core = lax.rem(rank, CORES)
@@ -303,7 +304,6 @@
 
     arrive_ahead(own_piece, own_recv.at[0])
     send_passed(own_piece, load_sem.at[8], own_recv.at[1])
-    arrive_pair(own_piece, own_recv.at[1])
 
     blank = jnp.zeros((LANES - full, obs_slots), BF16)
 
@@ -314,25 +314,28 @@
             block, wide, (((1,), (1,)), ((), ())), preferred_element_type=F32
         )
 
-    for s in range(LIVE_MAX):
-        product(s)
-
-    for side, offset in ((0, -1), (1, 1)):
-        source = me - offset
-
-        @pl.when((source >= 0) & (source < devices))
-        def _(copy=mig_copies[side]):
-            copy.wait_recv()
-
-    for s in [*range(early.stop, LIVE_MAX), *range(early.start)]:
-        position = new_start + s
-        left = mig_in[0, jnp.clip(position - old_start + MOVE, 0, MOVE - 1)]
-        own = back_t[jnp.clip(position - old_start, 0, capacity - 1)]
-        right = mig_in[1, jnp.clip(position - old_end, 0, MOVE - 1)]
-        row = jnp.where(position < old_start, left, jnp.where(position < old_end, own, right))
-        states[s, rank, :members] = row
-    for piece in (last_piece, first_piece):
-        send_own(piece, state_send, state_recv.at[0], state_recv.at[1])
+    def own_products():
+        arrive_pair(own_piece, own_recv.at[1])
+        for s in range(LIVE_MAX):
+            product(s)
+
+    def send_states():
+        for side, offset in ((0, -1), (1, 1)):
+            source = me - offset
+
+            @pl.when((source >= 0) & (source < devices))
+            def _(copy=mig_copies[side]):
+                copy.wait_recv()
+
+        for s in [*range(early.stop, LIVE_MAX), *range(early.start)]:
+            position = new_start + s
+            left = mig_in[0, jnp.clip(position - old_start + MOVE, 0, MOVE - 1)]
+            own = back_t[jnp.clip(position - old_start, 0, capacity - 1)]
+            right = mig_in[1, jnp.clip(position - old_end, 0, MOVE - 1)]
+            row = jnp.where(position < old_start, left, jnp.where(position < old_end, own, right))
+            states[s, rank, :members] = row
+        for piece in (last_piece, first_piece):
+            send_own(piece, state_send, state_recv.at[0], state_recv.at[1])
 
     def pass_far(g):
         arrive_ahead(far[g], far_recv.at[0, g])
@@ -345,6 +348,8 @@
 
     @pl.when(core == 0)
     def _():
+        own_products()
+        send_states()
         for g in range(HPEER):
             pass_far(g)
             far_products(g)
@@ -353,6 +358,8 @@
     def _():
         for g in range(HPEER):
             pass_far(g)
+        own_products()
+        send_states()
         for g in range(HPEER):
             far_products(g)
 
@@ -381,74 +388,97 @@
         high, low = cut(a)
         return jnp.concatenate([high, low], axis=1)
 
-    norms = []
-    for b in range(per_core):
-        slot = jnp.minimum(CORES * b + core, LIVE_MAX - 1)
-        gram = gram_s[slot]
-        for e in range(entries):
-            named = region_ref[e, slot]
-            index = jnp.where(named < capacity, named, named - capacity + LIVE_MAX)
-            index = jnp.clip(index, 0, LIVE_MAX + halo_count - 1)
-            gram += weight_ref[e, slot] * gram_s[index]
-        system = jnp.where(kept, gram, 0.0) + shift * unit
-        square = jnp.where(live, system * system, 0.0)
-        total = jnp.sum(jnp.sum(square, axis=1, keepdims=True), axis=0, keepdims=True)
-        norm = jnp.sqrt(total)
-        norms.append(norm)
-        y = system / norm
-        middle = half_unit - 0.5 * jnp.where(live, y, 0.0)
-        high, low = cut(middle)
-        first = times(wide(y), tall(high), tall(low))
-        yz_s[b, :full] = wide(jnp.where(rider, 0.0, first))
-        yz_s[b, full : 2 * full] = wide(jnp.where(rider, first, middle))
-
-    def cross(b):
-        z = yz_s[b, full : 2 * full]
-        return times(z, yz_s[b, :LANES, :LANES], yz_s[b, :LANES, LANES:])
-
-    def step(_, carry):
-        middles = []
-        for b in range(per_core):
+    def solve(first_slot, count):
+        norms = []
+        for b in range(count):
+            slot = first_slot + b
+            gram = gram_s[slot]
+            for e in range(entries):
+                named = region_ref[e, slot]
+                index = jnp.where(named < capacity, named, named - capacity + LIVE_MAX)
+                index = jnp.clip(index, 0, LIVE_MAX + halo_count - 1)
+                gram += weight_ref[e, slot] * gram_s[index]
+            system = jnp.where(kept, gram, 0.0) + shift * unit
+            square = jnp.where(live, system * system, 0.0)
+            total = jnp.sum(jnp.sum(square, axis=1, keepdims=True), axis=0, keepdims=True)
+            norm = jnp.sqrt(total)
+            norms.append(norm)
+            high, low = cut(jnp.where(live, system, 0.0))
+            squared = times(wide(system), tall(high), tall(low))
+            scale = 1.0 / norm
+            y = system * scale
+            middle = half_unit - 0.5 * jnp.where(live, y, 0.0)
+            first = 1.5 * y - (0.5 * scale * scale) * squared
+            yz_s[b, :full] = wide(jnp.where(rider, 0.0, first))
+            yz_s[b, full : 2 * full] = wide(jnp.where(rider, first, middle))
+
+        def cross(b):
+            z = yz_s[b, full : 2 * full]
+            return times(z, yz_s[b, :LANES, :LANES], yz_s[b, :LANES, LANES:])
+
+        def step(_, carry):
+            middles = []
+            for b in range(count):
+                high, low = cut(half_unit - 0.5 * cross(b))
+                middles.append((tall(high), tall(low)))
+            for b in range(count):
+                yz_s[b, : 2 * full] = wide(times(yz_s[b, : 2 * full], *middles[b]))
+            return carry
+
+        for k in range(NS_ITERS - 2):
+            step(k, 0)
+
+        piece = CORES * PAD
+        block = 16
+        start_row = members // block * block
+        middles, riders = [], []
+        for b in range(count):
             high, low = cut(half_unit - 0.5 * cross(b))
             middles.append((tall(high), tall(low)))
-        for b in range(per_core):
-            yz_s[b, : 2 * full] = wide(times(yz_s[b, : 2 * full], *middles[b]))
-        return carry
-
-    for k in range(NS_ITERS - 2):
-        step(k, 0)
-
-    piece = CORES * PAD
-    block = 16
-    start_row = members // block * block
-    middles, riders = [], []
-    for b in range(per_core):
-        high, low = cut(half_unit - 0.5 * cross(b))
-        middles.append((tall(high), tall(low)))
-        q = yz_s[b, full + start_row : full + start_row + block]
-        z_rows = slice(full, full + LANES)
-        riders.append(times(q, yz_s[b, z_rows, :LANES], yz_s[b, z_rows, LANES:]))
-    for b in range(per_core):
-        chosen = yz_s[b, pl.ds(pl.multiple_of(full + chip * piece, block), piece)]
-        stack = jnp.concatenate([chosen, wide(riders[b])], axis=0)
-        both = times(stack, *middles[b])
-        lead = times(wide(both[piece:]), *middles[b])[members - start_row : members - start_row + 1]
-        spread = math.sqrt(ensemble - 1) * lax.rsqrt(norms[b])
-        t_full[:, b] = (spread * both[:piece] + lead).astype(BF16).reshape(CORES, PAD, LANES)
-
-    other = 1 - core
-    t_copy = remote(t_full.at[other], t_all.at[core], t_send, t_recv, (me, pair))
-    t_copy.start()
-    t_all[core] = t_full[core]
+            q = yz_s[b, full + start_row : full + start_row + block]
+            z_rows = slice(full, full + LANES)
+            riders.append(times(q, yz_s[b, z_rows, :LANES], yz_s[b, z_rows, LANES:]))
+        for b in range(count):
+            chosen = yz_s[b, pl.ds(pl.multiple_of(full + chip * piece, block), piece)]
+            stack = jnp.concatenate([chosen, wide(riders[b])], axis=0)
+            both = times(stack, *middles[b])
+            lead = times(wide(both[piece:]), *middles[b])[members - start_row : members - start_row + 1]
+            spread = math.sqrt(ensemble - 1) * lax.rsqrt(norms[b])
+            t_full[:, first_slot + b] = (spread * both[:piece] + lead).astype(BF16).reshape(CORES, PAD, LANES)
+
+    def exchange(core_from):
+        rows = (0, SPLIT) if core_from == 0 else (SPLIT, LIVE_MAX)
+        target = t_full.at[1 - core_from, rows[0] : rows[1]]
+        return remote(target, t_all.at[rows[0] : rows[1]], t_send, t_recv, (me, pair))
+
+    @pl.when(core == 0)
+    def _():
+        solve(0, SPLIT)
+        exchange(0).start()
+        t_all[0:SPLIT] = t_full[0, 0:SPLIT]
+
+    @pl.when(core != 0)
+    def _():
+        solve(SPLIT, LIVE_MAX - SPLIT)
+        exchange(1).start()
+        t_all[SPLIT:LIVE_MAX] = t_full[1, SPLIT:LIVE_MAX]
 
     arrive_ahead(every_piece, state_recv.at[0])
     send_passed(every_piece, state_send, state_recv.at[1])
     arrive_pair(every_piece, state_recv.at[1])
 
     piece_row = lax.broadcasted_iota(jnp.int32, (PAD, full), 0)
-    t_copy.wait_recv()
+
+    @pl.when(core == 0)
+    def _():
+        exchange(1).wait_recv()
+
+    @pl.when(core != 0)
+    def _():
+        exchange(0).wait_recv()
+
     for s in range(LIVE_MAX):
-        weights = t_all[s % CORES, s // CORES][:, :full]
+        weights = t_all[s][:, :full]
         weights = jnp.where(piece_row == members, jnp.ones_like(weights), weights)
         keep = 1.0 - jnp.sum(weights.astype(F32), axis=1, keepdims=True)
         blended = dot(weights, states[s].reshape(full, width))
@@ -473,7 +503,15 @@
         def _(copy=mig_copies[side]):
             copy.wait_send()
 
-    t_copy.wait_send()
+
+    @pl.when(core == 0)
+    def _():
+        exchange(0).wait_send()
+
+    @pl.when(core != 0)
+    def _():
+        exchange(1).wait_send()
+
     whole_of(own_piece, load_sem.at[8], ranks - 1).wait()
     whole_of(every_piece, state_send, ranks - 1).wait()
     for g in range(HPEER):
@@ -486,7 +524,7 @@
     obs_slots = obs_ens.shape[2]
     full = PAD * ranks
     halo_count = HPEER * HCAP
-    per_core = -(-LIVE_MAX // CORES)
+    per_core = max(SPLIT, LIVE_MAX - SPLIT)
     hbm = pl.BlockSpec(memory_space=pltpu.MemorySpace.HBM)
     vmem = pl.BlockSpec(memory_space=pltpu.VMEM)
     count = len(OFFSETS)
@@ -510,8 +548,8 @@
             pltpu.VMEM((LIVE_MAX, ranks, PAD, width), BF16),
             pltpu.VMEM((LIVE_MAX + halo_count, full, LANES), F32),
             pltpu.VMEM((per_core, full + LANES, 2 * LANES), BF16),
-            pltpu.VMEM((CORES, per_core, PAD, LANES), BF16),
-            pltpu.VMEM((CORES, per_core, PAD, LANES), BF16),
+            pltpu.VMEM((CORES, LIVE_MAX, PAD, LANES), BF16),
+            pltpu.VMEM((LIVE_MAX, PAD, LANES), BF16),
             pltpu.SemaphoreType.REGULAR((REACH,)),
             dma((len(operands),)),
             dma((count,)),

time: 18.6 us -> 18.6 us (level)
  no operation moved by 1% of the time
where the time goes in v4:
time: 18.6 us; the launch traced here: 18.5 us
  Pallas kernels  17.6 us (95%)
  local copies, waits for them, and re-layouts  0.82 us (4%)
    pallas_call x1, Pallas kernels, shards(): pl.pallas_call(functools.partial(kernel, devices, ranks), out_shape=pltpu...  17.6 us
    pallas_call x1, local copies, waits for them, and re-layouts, shards(): pl.pallas_call(functools.partial(kernel, devices, ranks), out_shape=pltpu...  0.82 us

profile of v4, /device:TPU:25, one launch (start us, length us, event | category | flops | bytes accessed | tf_op | source)
XLA Modules:
  0.0 18.5 jit_solution(13179503870374509067)
XLA Ops:
  0.0 17.6 %shard_map.100 = bf16[14,20,512]{2,1,0:T(8,128)(2,1)S(1)} custom-call(s32[9]{0:T(128)} %old_hbm.1, s32[9]{0:T(128)} %new_hbm.1, s32[14]{0:T(128)} %count_hbm.1, s32[8,12]{1,0:T(8,128)} %halo_hbm.1, s32[7,14]{1,0:T(8,128)} %bitcast.6, f32[7,14]{1,0:T(8,128)} %bitcast.7, bf16[20,14,512]{2,1,0:T(8,128)(2,1)} %bitcast.4, bf16[20,14,128]{2,1,0:T(8,128)(2,1)} %bitcast.5, ...), custom_call_target="tpu_custom_call" | custom-call | flops 100000000 | bytes 10000000 | tf_op jit(solution)/shard_map/pallas_call | solution.py:535
  17.6 0.8 %copy.11 = bf16[14,20,512]{2,0,1:T(8,128)(2,1)} copy(bf16[14,20,512]{2,1,0:T(8,128)(2,1)S(1)} %shard_map.100) | data formatting | bytes 573440 | tf_op jit(solution)/shard_map/pallas_call | solution.py:535
